TPU v7x, 1024 devices: a whole 4x4x32 slice. The times are simulated.
1024 devices in a mesh: rows: 16 (over y, x), mp: 64 (over z, core).
Axes of the slice: x: 4, y: 4, z: 32, core: 2. Of those that a mesh axis runs over, the one named last changes fastest.
Arguments:
- tokens: bfloat16 [2048, 6144], P('rows', 'mp'), may hold values from -8 to 8
- norm_gain: float32 [6144], replicated, may hold values from 0.25 to 1.75
- hidden_bias: float32 [24576], P('mp'), may hold values from -3 to 3
- weight_in: bfloat16 [6144, 24576], P('rows', 'mp'), may hold values from -0.078125 to 0.078125
- weight_out: bfloat16 [24576, 6144], P('mp', 'rows'), may hold values from -0.109375 to 0.109375
Outputs:
- updated: bfloat16 [2048, 6144], P('rows', 'mp')
All inputs are finite; a program needn't handle non-finite values.
Results may differ from a plain program's by a relative error of at most 0.0041.
Values may be sent and summed in bfloat16 or wider, within the bound.
A program may use at most 64 MiB of HBM per device.

v0:
```python
import jax
import jax.numpy as jnp
from jax import lax
from jax.sharding import Mesh
from jax.sharding import PartitionSpec as P

D = 6144
MP = ("mp_0", "mp_1")
ROWS = ("rows_0", "rows_1")


floor_value = 0.1


def in_order(parts, dim):
    parts = jnp.moveaxis(parts, 0, dim)
    lengths = parts.shape
    return parts.reshape(*lengths[:dim], lengths[dim] * lengths[dim + 1], *lengths[dim + 2 :])


def all_blocks(array, axes, order):
    parts = array
    for k in order:
        parts = lax.all_gather(parts, axes[k])
    done = order[::-1]
    back = [done.index(k) for k in range(len(axes))]
    parts = parts.transpose(*back, *range(len(axes), parts.ndim))
    return parts.reshape(-1, *array.shape)


def gathered_by_axis(array, axes, order, dim):
    return in_order(all_blocks(array, axes, order), dim)


def summed_rows(subtotal, axes):
    for axis in axes:
        subtotal = lax.psum_scatter(subtotal, axis, scatter_dimension=0, tiled=True)
    return subtotal


def reduced_to_own(parts, axes, order):
    inside = parts.shape[1:]
    parts = parts.reshape(*(lax.axis_size(a) for a in axes), *inside)
    parts = jnp.moveaxis(parts, order, range(len(axes))).reshape(-1, *inside)
    for k in order:
        parts = lax.psum_scatter(parts, axes[k], scatter_dimension=0, tiled=True)
    return parts[0]


def cut_along(array, dim, peers):
    lengths = array.shape
    parts = array.reshape(*lengths[:dim], peers, lengths[dim] // peers, *lengths[dim + 1 :])
    return jnp.moveaxis(parts, dim, 0)


def sum_by_axis(array, axes, order, dim):
    peers = lax.axis_size(axes)
    return reduced_to_own(cut_along(array, dim, peers), axes, order)


def normalize(as_float, moment_sum, square_sum, gain, width):
    row_mean = moment_sum / width
    row_var = jnp.maximum(square_sum / width - row_mean * row_mean, 0.0)
    inverse = lax.rsqrt(row_var + floor_value)
    return ((as_float - row_mean[:, None]) * inverse[:, None] * gain[None, :]).astype(jnp.bfloat16)


def body(tokens, norm_gain, hidden_bias, weight_in, weight_out):
    as_float = tokens.astype(jnp.float32)
    gathered = gathered_by_axis(tokens, MP, (0, 1), 1).astype(jnp.float32)
    normed = normalize(
        gathered, jnp.sum(gathered, axis=1), jnp.sum(gathered * gathered, axis=1), norm_gain, D
    )
    shuffled = lax.all_to_all(normed, ROWS, split_axis=1, concat_axis=0, tiled=True)
    preact = summed_rows(jnp.dot(shuffled, weight_in, preferred_element_type=jnp.float32), ROWS)
    hidden = jax.nn.gelu(preact + hidden_bias[None, :], approximate=False).astype(jnp.bfloat16)
    terms = jnp.dot(
        hidden,
        lax.all_gather(weight_out, ROWS, axis=1, tiled=True),
        preferred_element_type=jnp.float32,
    )
    branch = sum_by_axis(terms, MP, (1, 0), 1)
    return (as_float + branch).astype(jnp.bfloat16)


def solution(mesh):
    finer = Mesh(mesh.devices.reshape(4, 4, 32, 2), ("rows_0", "rows_1", "mp_0", "mp_1"))
    placed = (P(ROWS, MP), P(), P(MP), P(ROWS, MP), P(MP, ROWS))
    return jax.shard_map(body, mesh=finer, in_specs=placed, out_specs=P(ROWS, MP), check_vma=False)
```

profile of v0, /device:TPU:6, one launch (start us, length us, event | category | flops | bytes accessed | tf_op | source)
XLA Modules:
  0.0 444.3 jit_solution(7556846284784996967)
XLA Ops:
  7.4 72.8 %all-gather = bf16[4096,96]{0,1:T(8,128)(2,1)S(1)} all-gather(bf16[128,96]{0,1:T(8,128)(2,1)} %param.5), channel_id=2, replica_groups=mesh['rows_0'=4,'rows_1'=4,'mp_0'=32,'mp_1'=2] {'mp_0'}, dimensions={0}, use_global_device_ids=true | all-gather | bytes 811008 | tf_op jit(solution)/shard_map/all_gather | solution.py:24
  80.2 1.0 copy.21
  81.2 0.0 reduce-scatter.5.cloned.1.call-start
  81.3 22.6 %all-gather.7.cloned.1.call-done = bf16[64,128,96]{1,0,2:T(8,128)(2,1)} async-done(((bf16[32,128,96]{1,0,2:T(8,128)(2,1)}), bf16[64,128,96]{1,0,2:T(8,128)(2,1)}) %all-gather.7.cloned.1.call-update) | async-done | bytes 1572880 | tf_op jit(solution)/shard_map/all_gather | solution.py:24
  103.9 2.4 copy.14
  106.3 0.8 multiply_reduce_fusion
  107.1 0.4 convert_element_type.54
  107.5 1.8 copy.15
  109.3 0.8 convert_reduce_fusion
  110.2 1.0 multiply_convert_fusion
  111.2 27.7 %all_to_all.16 = bf16[128,16,384]{0,2,1:T(8,128)(2,1)S(1)} all-to-all(bf16[128,16,384]{0,2,1:T(8,128)(2,1)S(1)} %multiply_convert_fusion), channel_id=1, replica_groups=mesh['rows_0'=4,'rows_1'=4,'mp_0'=32,'mp_1'=2] {'rows_0','rows_1'}, dimensions={1} | all-to-all | bytes 3145728 | tf_op jit(solution)/shard_map/all_to_all | solution.py:74
  138.8 0.9 copy.16
  139.7 2.8 fusion.74
  142.5 0.0 all-gather.5.cloned.1.call-start
  142.5 0.5 all-gather.5.cloned.1.call-update
  143.1 59.1 %reduce-scatter.5.cloned.1.call-done = f32[512,384]{1,0:T(8,128)} async-done(((f32[2048,384]{1,0:T(8,128)}), f32[512,384]{1,0:T(8,128)}) %reduce-scatter.5.cloned.1.call-update) | async-done | bytes 786448 | tf_op jit(solution)/shard_map/reduce_scatter | solution.py:37
  202.3 54.4 %all-gather.5.cloned.1.call-done = bf16[384,6144]{1,0:T(8,128)(2,1)} async-done(((bf16[384,384]{1,0:T(8,128)(2,1)}), bf16[384,6144]{1,0:T(8,128)(2,1)}) %all-gather.5.cloned.1.call-update) | async-done | bytes 4718608 | tf_op jit(solution)/shard_map/all_gather | solution.py:79
  256.6 1.0 reduce-scatter.7.cloned.1.call-done
  257.7 4.6 %fusion.10 = f32[128,6144]{0,1:T(8,128)S(1)} fusion(bf16[384,6144]{1,0:T(8,128)(2,1)} %all-gather.5.cloned.1.call-done, f32[128,384]{1,0:T(8,128)} %reduce-scatter.7.cloned.1.call-done, f32[384]{0:T(512)S(1)} %copy-done.4), kind=kOutput, calls=%fused_computation.22 | convolution fusion | flops 607223808 | bytes 8062464 | tf_op jit(solution)/shard_map/dot_general | solution.py:77
  262.3 1.9 copy.18
  264.2 0.0 reduce-scatter.11.cloned.1.call-start
  264.3 32.5 %reduce-scatter.9.cloned.1.call-done = f32[32,128,96]{1,2,0:T(8,128)} async-done(((f32[64,128,96]{1,2,0:T(8,128)}), f32[32,128,96]{1,2,0:T(8,128)}) %reduce-scatter.9.cloned.1.call-update) | async-done | bytes 1572880 | tf_op jit(solution)/shard_map/reduce_scatter | solution.py:46
  296.8 138.9 %reduce-scatter.11.cloned.1.call-done = f32[1,128,96]{1,2,0:T(8,128)} async-done(((f32[32,128,96]{1,2,0:T(8,128)}), f32[1,128,96]{1,2,0:T(8,128)}) %reduce-scatter.11.cloned.1.call-update) | async-done | bytes 49168 | tf_op jit(solution)/shard_map/reduce_scatter | solution.py:46
  435.7 1.4 fusion.43
  (20 shorter events, 0.2 us)
Async XLA Ops:
  7.4 132.3 %copy-start = (bf16[384,384]{1,0:T(8,128)(2,1)S(1)}, bf16[384,384]{1,0:T(8,128)(2,1)}, u32[]{:S(2)}) copy-start(bf16[384,384]{1,0:T(8,128)(2,1)} %param.8) | copy-start | bytes 884740
  7.4 73.9 %copy-start.3 = (f32[6144]{0:T(1024)S(1)}, f32[6144]{0:T(1024)}, u32[]{:S(2)}) copy-start(f32[6144]{0:T(1024)} %param.6) | copy-start | bytes 73732
  7.4 96.5 %all-gather.7.cloned.1.call-start = ((), (), s32[]{:S(2)}) async-start(), calls=%async_computation.10 | async-start | bytes 2359296 | tf_op jit(solution)/shard_map/all_gather | solution.py:24
  81.2 121.0 %reduce-scatter.5.cloned.1.call-start = ((), (), s32[]{:S(2)}) async-start(), calls=%async_computation.5 | async-start | bytes 3932160 | tf_op jit(solution)/shard_map/reduce_scatter | solution.py:37
  103.9 3.3 copy-start.1
  142.5 115.2 %copy-start.4 = (f32[384]{0:T(512)S(1)}, f32[384]{0:T(512)}, u32[]{:S(2)}) copy-start(f32[384]{0:T(512)} %param.7) | copy-start | bytes 4612
  142.5 114.2 %all-gather.5.cloned.1.call-start = ((), (), s32[]{:S(2)}) async-start(), calls=%async_computation.7 | async-start | bytes 5013504 | tf_op jit(solution)/shard_map/all_gather | solution.py:79
  143.1 114.6 %reduce-scatter.7.cloned.1.call-start = ((), (), s32[]{:S(2)}) async-start(), calls=%async_computation.6 | async-start | bytes 983040 | tf_op jit(solution)/shard_map/reduce_scatter | solution.py:37
  202.2 94.6 %reduce-scatter.9.cloned.1.call-start = ((), (), s32[]{:S(2)}) async-start(), calls=%async_computation.8 | async-start | bytes 4718592 | tf_op jit(solution)/shard_map/reduce_scatter | solution.py:46
  264.2 171.6 %copy-start.2 = (bf16[128,96]{0,1:T(8,128)(2,1)S(1)}, bf16[128,96]{0,1:T(8,128)(2,1)}, u32[]{:S(2)}) copy-start(bf16[128,96]{0,1:T(8,128)(2,1)} %param.5) | copy-start | bytes 73732
  264.2 171.5 %reduce-scatter.11.cloned.1.call-start = ((), (), s32[]{:S(2)}) async-start(), calls=%async_computation.9 | async-start | bytes 1622016 | tf_op jit(solution)/shard_map/reduce_scatter | solution.py:46
Sparse Core Ops, SparseCore 0:
  81.3 22.4 all-gather.6
  142.6 59.5 reduce-scatter.4
  205.6 51.9 reduce-scatter.6
  264.3 32.4 reduce-scatter.8
Sparse Core Ops, SparseCore 1:
  147.1 109.5 all-gather.4
  296.9 138.8 reduce-scatter.10
where the time goes:
time: 445 us; the launch traced here: 444 us
  waiting for transfers between devices  309 us (69%)
  blocking collectives  100 us (22%)
  between operations  14.6 us (3%)
  local copies, waits for them, and re-layouts  8.09 us (2%)
  matrix products  7.37 us (2%)
    reduce_scatter x2, waiting for transfers between devices, reduced_to_own(): parts = lax.psum_scatter(parts, axes[k], scatter_dimension=0, tiled=True)  171 us
    all_gather x1, blocking collectives, all_blocks(): parts = lax.all_gather(parts, axes[k])  72.8 us
    reduce_scatter x2, waiting for transfers between devices, summed_rows(): subtotal = lax.psum_scatter(subtotal, axis, scatter_dimension=0, tiled=True)  60.1 us
    all_gather x1, waiting for transfers between devices, body(): lax.all_gather(weight_out, ROWS, axis=1, tiled=True)  54.4 us
    all_to_all x1, blocking collectives, body(): lax.all_to_all(normed, ROWS, split_axis=1, concat_axis=0, tiled=True)  27.7 us
    all_gather x1, waiting for transfers between devices, all_blocks(): parts = lax.all_gather(parts, axes[k])  22.6 us
  transfers between devices with their start and end apart: 6, of which 6 were waited for; matrix products, arithmetic and copies ran while one was open for 0% of the time, Pallas kernels for 0%

commit v1 on v0

v1 whole, which is shorter than its diff:
```python
import jax
import jax.numpy as jnp
from jax import lax
from jax.experimental import pallas as pl
from jax.experimental.pallas import tpu as pltpu
from jax.sharding import Mesh
from jax.sharding import PartitionSpec as P

MP = ("mp_0", "mp_1")
ROWS = ("rows_0", "rows_1")
NZ = 32
NP = 4
NR = 16
TOK = 128
FEAT = 96
BLK = 384
HALF = 192
WIDTH = NZ * 2 * FEAT
STEPS = NZ // 2
F32 = jnp.float32
BF16 = jnp.bfloat16

floor_value = 0.1


def gelu(v):
    return 0.5 * v * (1.0 + lax.erf(v * 0.7071067811865476))


def kernel(
    tok_ref, gain_ref, bias_ref, win_ref, wout_ref, out_ref,
    xt, nx, w1, w2, gt, hid, pad, rsin, rsout, res, part,
    ag_send, ag_recv, push_send, own_send, own_recv,
    pl_send, pl_recv, wp_send, wp_recv, nb_send, nb_recv,
    hid_send, hid_recv, rs_send, rs_recv, res_send, res_recv,
):
    y = lax.axis_index("rows_0")
    x = lax.axis_index("rows_1")
    z = lax.axis_index("mp_0")
    c = lax.axis_index("mp_1")
    r = y * NP + x

    def dev(yy, xx, zz, cc):
        return (yy, xx, zz, cc)

    partner = dev(y, x, z, 1 - c)
    zup = dev(y, x, (z + 1) % NZ, c)
    zdn = dev(y, x, (z + NZ - 1) % NZ, c)

    def remote(src, dst, ssem, rsem, to):
        return pltpu.make_async_remote_copy(
            src_ref=src, dst_ref=dst, send_sem=ssem, recv_sem=rsem,
            device_id=to, device_id_type=pl.DeviceIdType.MESH,
        )

    def signal_all(targets):
        bar = pltpu.get_barrier_semaphore()
        for t in targets:
            pl.semaphore_signal(bar, inc=1, device_id=t, device_id_type=pl.DeviceIdType.MESH)

    def wait_all(n):
        pl.semaphore_wait(pltpu.get_barrier_semaphore(), n)

    xup = dev(y, (x + 1) % NP, z, c)
    xdn = dev(y, (x + NP - 1) % NP, z, c)
    yup = dev((y + 1) % NP, x, z, c)
    ydn = dev((y + NP - 1) % NP, x, z, c)

    @pl.when(c == 0)
    def _():
        signal_all([partner, xup, xdn, yup, ydn])

    @pl.when(c == 1)
    def _():
        signal_all([partner, zup, zdn])

    pad[...] = jnp.zeros((128, 128), F32)
    pad[:, 0:FEAT] = tok_ref[...].astype(F32)
    xt[z, c] = pad[...].T[0:FEAT, :].astype(BF16)

    def put_weight(src, dst):
        t = src[...].astype(F32).T.astype(BF16)
        dst[c, 2 * r] = t[0:HALF, :]
        dst[c, 2 * r + 1] = t[HALF:BLK, :]

    def spread_gain(t):
        row = gain_ref[pl.ds(t, 1), :]
        gt[t] = jnp.broadcast_to(row, (128, 128)).T

    def bias_column():
        parts = [jnp.broadcast_to(bias_ref[k:k + 1, :], (128, 128)).T for k in range(3)]
        return jnp.concatenate(parts, axis=0)

    def hidden(cc):
        def stat(j, carry):
            s, q = carry
            v = xt[j].reshape(HALF, TOK).astype(F32)
            return s + jnp.sum(v, axis=0, keepdims=True), q + jnp.sum(v * v, axis=0, keepdims=True)

        zero = jnp.zeros((1, TOK), F32)
        s, q = lax.fori_loop(0, NZ, stat, (zero, zero))
        mean = s / WIDTH
        var = jnp.maximum(q / WIDTH - mean * mean, 0.0)
        inv = lax.rsqrt(var + floor_value)

        def norm(j, _):
            v = xt[pl.ds(2 * j, 2)].reshape(BLK, TOK).astype(F32)
            g = gt[pl.ds(3 * j, 3)].reshape(BLK, TOK)
            nx[j] = ((v - mean) * inv * g).astype(BF16)
            return 0

        lax.fori_loop(0, NR, norm, 0)
        return None

    def project(cc):
        def step(j, acc):
            w = w1[cc, pl.ds(2 * j, 2)].reshape(BLK, BLK)
            return acc + jnp.dot(w, nx[j], preferred_element_type=F32)

        acc = lax.fori_loop(0, NR, step, jnp.zeros((BLK, TOK), F32))
        hid[cc] = gelu(acc + bias_column()).astype(BF16)

    @pl.when(c == 0)
    def _():
        weights = (w1, w2)

        def full(w, cc, b):
            return weights[w].at[cc, pl.ds(2 * b, 2)]

        def half(w, cc, b, h):
            return weights[w].at[cc, 2 * b + h]

        def axis(cc):
            if cc == 0:
                return x, y, (lambda p, q: q * NP + p), (lambda p, q: dev(q, p, z, c))
            return y, x, (lambda p, q: p * NP + q), (lambda p, q: dev(p, q, z, c))

        def send(w, cc, ref, idx, to):
            remote(ref, ref, pl_send.at[w, cc], pl_recv.at[w, cc, idx], to).start()

        def arrived(w, cc, ref, idx):
            remote(ref, ref, pl_send.at[w, cc], pl_recv.at[w, cc, idx], partner).wait_recv()

        def push(w, cc, b):
            if w == 0 and cc == 0:
                return
            ref = full(w, cc, b)
            remote(ref, ref, wp_send.at[w, cc], wp_recv.at[w, cc, b], partner).start()

        def mod(v):
            return (v + NP) % NP

        offs = (0, -1, 1, 2)

        def own_sends(w, pred):
            @pl.when(pred(r))
            def _():
                for cc in (0, 1):
                    p, q, ident, at = axis(cc)
                    send(w, cc, full(w, cc, r), 0, at(mod(p + 1), q))
                    send(w, cc, full(w, cc, r), 1, at(mod(p - 1), q))
                for cc in (0, 1):
                    p, q, ident, at = axis(cc)
                    send(w, cc, full(w, cc, r), 4, at(p, mod(q + 1)))
                    send(w, cc, full(w, cc, r), 5, at(p, mod(q - 1)))
                if w == 1:
                    push(w, 0, r)

        def q_sends(w, cc, i, b):
            p, q, ident, at = axis(cc)
            send(w, cc, full(w, cc, b), 4 + 4 * i, at(p, mod(q + 1)))
            send(w, cc, full(w, cc, b), 5 + 4 * i, at(p, mod(q - 1)))

        def first_full(w, pred):
            for d in (0, 1):
                for cc in (0, 1):
                    p, q, ident, at = axis(cc)
                    b = ident(mod(p - 1), q) if d == 0 else ident(mod(p + 1), q)

                    @pl.when(pred(b))
                    def _():
                        arrived(w, cc, full(w, cc, b), d)
                        to = at(mod(p + 1), q) if d == 0 else at(mod(p - 1), q)
                        send(w, cc, half(w, cc, b, d), 2 + d, to)
                        q_sends(w, cc, 1 + d, b)
                        push(w, cc, b)

        def first_half(w, pred):
            for cc in (0, 1):
                p, q, ident, at = axis(cc)
                b = ident(mod(p + 2), q)

                @pl.when(pred(b))
                def _():
                    arrived(w, cc, half(w, cc, b, 0), 2)
                    arrived(w, cc, half(w, cc, b, 1), 3)
                    q_sends(w, cc, 3, b)
                    push(w, cc, b)

        def second_full(w, pred, i):
            for d in (0, 1):
                for cc in (0, 1):
                    p, q, ident, at = axis(cc)
                    b = ident(mod(p + offs[i]), mod(q - 1) if d == 0 else mod(q + 1))

                    @pl.when(pred(b))
                    def _():
                        arrived(w, cc, full(w, cc, b), 4 + 4 * i + d)
                        to = at(p, mod(q + 1)) if d == 0 else at(p, mod(q - 1))
                        send(w, cc, half(w, cc, b, d), 6 + 4 * i + d, to)
                        push(w, cc, b)

        def second_half(w, pred, i):
            for cc in (0, 1):
                p, q, ident, at = axis(cc)
                b = ident(mod(p + offs[i]), mod(q + 2))

                @pl.when(pred(b))
                def _():
                    arrived(w, cc, half(w, cc, b, 0), 6 + 4 * i)
                    arrived(w, cc, half(w, cc, b, 1), 7 + 4 * i)
                    push(w, cc, b)

        def events(w, pred):
            first_full(w, pred)
            second_full(w, pred, 0)
            first_half(w, pred)
            second_full(w, pred, 1)
            second_full(w, pred, 2)
            second_half(w, pred, 0)
            second_full(w, pred, 3)
            second_half(w, pred, 1)
            second_half(w, pred, 2)
            second_half(w, pred, 3)

        def every(b):
            return b >= 0

        def far(b):
            return (b - z // 2 - 4 + 2 * NR) % NR < NR // 2

        def near(b):
            return (b - z // 2 - 4 + 2 * NR) % NR >= NR // 2

        put_weight(win_ref, w1)
        wait_all(5)
        remote(xt.at[z, 0], xt.at[z, 0], own_send, own_recv, partner).start()
        remote(full(0, 1, r), full(0, 1, r), nb_send.at[0], nb_recv.at[0], partner).wait_recv()
        own_sends(0, every)
        put_weight(wout_ref, w2)
        lax.fori_loop(0, 48, lambda t, _: (spread_gain(t), 0)[1], 0)
        events(0, every)
        remote(full(1, 1, r), full(1, 1, r), nb_send.at[1], nb_recv.at[1], partner).wait_recv()
        own_sends(1, far)

        remote(xt.at[z, 1], xt.at[z, 1], own_send, own_recv, partner).wait_recv()

        def take(s, _):
            for h in (1, 0):
                a = (z + NZ - s) % NZ
                remote(xt.at[a, h], xt.at[a, h], push_send, ag_recv.at[0, s, h], partner).wait_recv()

                @pl.when(s < STEPS)
                def _():
                    b = (z + s) % NZ
                    remote(xt.at[b, h], xt.at[b, h], push_send, ag_recv.at[1, s, h], partner).wait_recv()

            return 0

        lax.fori_loop(1, STEPS + 1, take, 0)
        hidden(0)
        project(0)
        remote(hid.at[0], hid.at[0], hid_send, hid_recv, partner).start()
        events(1, far)
        own_sends(1, near)
        events(1, near)

        for w in (0, 1):
            for cc in (0, 1):
                ref = weights[w].at[cc, pl.ds(0, 30)]
                remote(ref, ref, pl_send.at[w, cc], pl_recv.at[w, cc, 0], partner).wait_send()
                if w == 1 and cc == 0:
                    ref = weights[w].at[cc, pl.ds(0, 32)]
                if w == 1 or cc == 1:
                    remote(ref, ref, wp_send.at[w, cc], wp_recv.at[w, cc, 0], partner).wait_send()
        remote(xt.at[z, 0], xt.at[z, 0], own_send, own_recv, partner).wait_send()
        remote(hid.at[0], hid.at[0], hid_send, hid_recv, partner).wait_send()
        remote(res.at[0], res.at[0], res_send, res_recv, partner).wait_recv()
        pad[0:FEAT, :] = res[0].astype(F32)

    @pl.when(c == 1)
    def _():
        wait_all(3)
        own1 = xt.at[z, 1]
        remote(own1, own1, ag_send, ag_recv.at[0, 1, 1], zup).start()
        remote(own1, own1, ag_send, ag_recv.at[1, 1, 1], zdn).start()
        remote(own1, own1, own_send, own_recv, partner).start()
        own0 = xt.at[z, 0]
        remote(own0, own0, own_send, own_recv, partner).wait_recv()
        remote(own0, own0, ag_send, ag_recv.at[0, 1, 0], zup).start()
        remote(own0, own0, ag_send, ag_recv.at[1, 1, 0], zdn).start()
        put_weight(win_ref, w1)
        wb = w1.at[1, pl.ds(2 * r, 2)]
        remote(wb, wb, nb_send.at[0], nb_recv.at[0], partner).start()

        def ring(s, _):
            for h in (1, 0):
                a = (z + NZ - s) % NZ
                ra = xt.at[a, h]
                remote(ra, ra, ag_send, ag_recv.at[0, s, h], zup).wait_recv()

                @pl.when(s < STEPS)
                def _():
                    remote(ra, ra, ag_send, ag_recv.at[0, s + 1, h], zup).start()

                remote(ra, ra, push_send, ag_recv.at[0, s, h], partner).start()

                @pl.when(s < STEPS)
                def _():
                    b = (z + s) % NZ
                    rb = xt.at[b, h]
                    remote(rb, rb, ag_send, ag_recv.at[1, s, h], zdn).wait_recv()

                    @pl.when(s < STEPS - 1)
                    def _():
                        remote(rb, rb, ag_send, ag_recv.at[1, s + 1, h], zdn).start()

                    remote(rb, rb, push_send, ag_recv.at[1, s, h], partner).start()

            for k in range(3):
                spread_gain(3 * (s - 1) + k)
            return 0

        ring(1, 0)
        put_weight(wout_ref, w2)
        wo = w2.at[1, pl.ds(2 * r, 2)]
        remote(wo, wo, nb_send.at[1], nb_recv.at[1], partner).start()
        lax.fori_loop(2, STEPS + 1, ring, 0)
        hidden(1)

        def take_weight(b, _):
            @pl.when(b != r)
            def _():
                ref = w1.at[1, pl.ds(2 * b, 2)]
                remote(ref, ref, wp_send.at[0, 1], wp_recv.at[0, 1, b], partner).wait_recv()

            return 0

        lax.fori_loop(0, NR, take_weight, 0)
        project(1)
        remote(hid.at[0], hid.at[0], hid_send, hid_recv, partner).wait_recv()

        def take_out(b):
            ra = w2.at[0, pl.ds(2 * b, 2)]
            remote(ra, ra, wp_send.at[1, 0], wp_recv.at[1, 0, b], partner).wait_recv()

            @pl.when(b != r)
            def _():
                rb = w2.at[1, pl.ds(2 * b, 2)]
                remote(rb, rb, wp_send.at[1, 1], wp_recv.at[1, 1, b], partner).wait_recv()

        def partial(d):
            return jnp.dot(w2[0, d], hid[0], preferred_element_type=F32) + jnp.dot(
                w2[1, d], hid[1], preferred_element_type=F32
            )

        def rs_copy(dr, s, h, to):
            return remote(
                rsout.at[dr, s, h], rsin.at[dr, s, h],
                rs_send.at[dr], rs_recv.at[dr, s, h], to,
            )

        def reduce(s, _):
            du = (z + STEPS - s) % NZ
            dd = (z + NZ - STEPS + 1 + s) % NZ

            @pl.when((s == 0) | (du % 2 == 1))
            def _():
                take_out(du // 2)

            part[0] = partial(du)

            @pl.when((s < STEPS - 1) & (dd % 2 == 0))
            def _():
                take_out(dd // 2)

            @pl.when(s < STEPS - 1)
            def _():
                part[1] = partial(dd)

            for h in (0, 1):
                rows = slice(FEAT * h, FEAT * h + FEAT)

                @pl.when(s > 0)
                def _():
                    rs_copy(0, s - 1, h, zup).wait_recv()
                    rsout[0, s, h] = (part[0, rows] + rsin[0, s - 1, h].astype(F32)).astype(BF16)

                @pl.when(s == 0)
                def _():
                    rsout[0, s, h] = part[0, rows].astype(BF16)

                rs_copy(0, s, h, zup).start()

                @pl.when((s > 0) & (s < STEPS - 1))
                def _():
                    rs_copy(1, s - 1, h, zdn).wait_recv()
                    rsout[1, s, h] = (part[1, rows] + rsin[1, s - 1, h].astype(F32)).astype(BF16)

                @pl.when(s == 0)
                def _():
                    rsout[1, s, h] = part[1, rows].astype(BF16)

                @pl.when(s < STEPS - 1)
                def _():
                    rs_copy(1, s, h, zdn).start()

            return 0

        lax.fori_loop(0, STEPS, reduce, 0)
        mine = partial(z)
        for h in (0, 1):
            rs_copy(0, STEPS - 1, h, zup).wait_recv()
            rs_copy(1, STEPS - 2, h, zdn).wait_recv()
            total = (
                xt[z, h].astype(F32)
                + mine[FEAT * h:FEAT * h + FEAT]
                + rsin[0, STEPS - 1, h].astype(F32)
                + rsin[1, STEPS - 2, h].astype(F32)
            )
            if h == 0:
                res[0] = total.astype(BF16)
                remote(res.at[0], res.at[0], res_send, res_recv, partner).start()
            else:
                pad[0:FEAT, :] = total

        remote(xt.at[pl.ds(0, NZ - 1)], xt.at[pl.ds(0, NZ - 1)], ag_send, own_recv, partner).wait_send()
        remote(xt.at[pl.ds(0, NZ - 1)], xt.at[pl.ds(0, NZ - 1)], push_send, own_recv, partner).wait_send()
        remote(own1, own1, own_send, own_recv, partner).wait_send()
        for w, ref in ((0, wb), (1, wo)):
            remote(ref, ref, nb_send.at[w], nb_recv.at[w], partner).wait_send()
        for dr, n in ((0, STEPS), (1, STEPS - 1)):
            ref = rsout.at[dr, pl.ds(0, n)]
            remote(ref, ref, rs_send.at[dr], own_recv, partner).wait_send()
        remote(res.at[0], res.at[0], res_send, res_recv, partner).wait_send()

    out_ref[...] = pad[...].T[:, 0:FEAT].astype(BF16)


def body(tokens, norm_gain, hidden_bias, weight_in, weight_out):
    dma = pltpu.SemaphoreType.DMA
    vmem = pl.BlockSpec(memory_space=pltpu.VMEM)
    return pl.pallas_call(
        kernel,
        out_shape=jax.ShapeDtypeStruct((TOK, FEAT), BF16),
        in_specs=[vmem] * 5,
        out_specs=vmem,
        scratch_shapes=[
            pltpu.VMEM((NZ, 2, FEAT, TOK), BF16),
            pltpu.VMEM((NR, BLK, TOK), BF16),
            pltpu.VMEM((2, NZ, HALF, BLK), BF16),
            pltpu.VMEM((2, NZ, HALF, BLK), BF16),
            pltpu.VMEM((48, 128, 128), F32),
            pltpu.VMEM((2, BLK, TOK), BF16),
            pltpu.VMEM((128, 128), F32),
            pltpu.VMEM((2, STEPS, 2, FEAT, TOK), BF16),
            pltpu.VMEM((2, STEPS, 2, FEAT, TOK), BF16),
            pltpu.VMEM((1, FEAT, TOK), BF16),
            pltpu.VMEM((2, HALF, TOK), F32),
            dma, dma((2, STEPS + 1, 2)), dma, dma, dma,
            dma((2, 2)), dma((2, 2, 20)), dma((2, 2)), dma((2, 2, NR)), dma((2,)), dma((2,)),
            dma, dma, dma((2,)), dma((2, STEPS, 2)), dma, dma,
        ],
        compiler_params=pltpu.CompilerParams(
            collective_id=0, has_side_effects=True, vmem_limit_bytes=60 * 1024 * 1024
        ),
    )(
        tokens,
        norm_gain.reshape(48, 128),
        hidden_bias.reshape(3, 128),
        weight_in,
        weight_out,
    )


def solution(mesh):
    finer = Mesh(mesh.devices.reshape(4, 4, 32, 2), ("rows_0", "rows_1", "mp_0", "mp_1"))
    placed = (P(ROWS, MP), P(), P(MP), P(ROWS, MP), P(MP, ROWS))
    return jax.shard_map(body, mesh=finer, in_specs=placed, out_specs=P(ROWS, MP), check_vma=False)
```

time: 445 us -> 145 us (0.33)
  waiting for transfers between devices: 309 us -> 0 us
  Pallas kernels: 0 us -> 140 us
  blocking collectives: 100 us -> 0 us
  between operations: 14.6 us -> 0.01 us
  matrix products: 7.37 us -> 0 us
  local copies, waits for them, and re-layouts: 8.09 us -> 2.9 us
    reduce_scatter x4 -> x0, waiting for transfers between devices: 232 us -> none  [the longest x2 171 us: reduced_to_own(): parts = lax.psum_scatter(parts, axes[k], scatter_dimension=0, tiled=True)]
    pallas_call x0 -> x1, Pallas kernels: none -> 140 us  [body(): pl.pallas_call(kernel, out_shape=jax.ShapeDtypeStruct((TOK, FEAT), BF16),...]
    all_gather x2 -> x0, waiting for transfers between devices: 76.9 us -> none  [the longest x1 54.4 us: body(): lax.all_gather(weight_out, ROWS, axis=1, tiled=True)]
    all_gather x1 -> x0, blocking collectives: 72.8 us -> none  [all_blocks(): parts = lax.all_gather(parts, axes[k])]
    all_to_all x1 -> x0, blocking collectives: 27.7 us -> none  [body(): lax.all_to_all(normed, ROWS, split_axis=1, concat_axis=0, tiled=True)]
    dot_general x2 -> x0, matrix products: 7.37 us -> none  [the longest x1 4.62 us: body(): jnp.dot(hidden, lax.all_gather(weight_out, ROWS, axis=1, tiled=True), pre...]
  transfers between devices with their start and end apart: 6 -> 0, of which waited for: 6 -> 0; matrix products, arithmetic and copies ran while one was open for 0% -> 0% of each run, Pallas kernels for 0% -> 0%
where the time goes in v1:
time: 145 us; the launch traced here: 143 us
  Pallas kernels  140 us (97%)
  local copies, waits for them, and re-layouts  2.9 us (2%)
    pallas_call x1, Pallas kernels, body(): pl.pallas_call(kernel, out_shape=jax.ShapeDtypeStruct((TOK, FEAT), BF16),...  140 us

profile of v1, /device:TPU:6, one launch (start us, length us, event | category | flops | bytes accessed | tf_op | source)
XLA Modules:
  0.0 143.4 jit_solution(15928413314577446277)
XLA Ops:
  0.0 1.4 %copy.6.tok_ref = bf16[128,96]{1,0:T(8,128)(2,1)} copy(bf16[128,96]{0,1:T(8,128)(2,1)} %param.5) | data formatting | bytes 49152 | tf_op args[0]
  1.4 140.5 %shard_map.55 = bf16[128,96]{1,0:T(8,128)(2,1)} custom-call(bf16[128,96]{1,0:T(8,128)(2,1)} %copy.6.tok_ref, f32[48,128]{1,0:T(8,128)} %bitcast.2, f32[3,128]{1,0:T(4,128)} %bitcast.3, bf16[384,384]{1,0:T(8,128)(2,1)} %win_ref.1, bf16[384,384]{1,0:T(8,128)(2,1)} %wout_ref.1), custom_call_target="tpu_custom_call" | custom-call | tf_op jit(solution)/shard_map/pallas_call | solution.py:453
  141.9 1.5 %copy.7 = bf16[128,96]{0,1:T(8,128)(2,1)} copy(bf16[128,96]{1,0:T(8,128)(2,1)} %shard_map.55) | data formatting | bytes 49152 | tf_op jit(solution)/shard_map/pallas_call | solution.py:453

commit v2 on v0

v2 whole, which is shorter than its diff:
```python
import jax
import jax.numpy as jnp
from jax import lax
from jax.experimental import pallas as pl
from jax.experimental.pallas import tpu as pltpu
from jax.sharding import Mesh
from jax.sharding import PartitionSpec as P

MP = ("mp_0", "mp_1")
ROWS = ("rows_0", "rows_1")
NZ = 32
NP = 4
NR = 16
TOK = 128
FEAT = 96
BLK = 384
HALF = 192
WIDTH = NZ * 2 * FEAT
STEPS = NZ // 2
PAIRS = STEPS // 2
F32 = jnp.float32
BF16 = jnp.bfloat16

floor_value = 0.1


def gelu(v):
    return 0.5 * v * (1.0 + lax.erf(v * 0.7071067811865476))


def kernel(
    tok_ref, gain_ref, bias_ref, win_ref, wout_ref, out_ref,
    xt, x4, nx, w1, w2, gt, st, sums, pout, pin, hid, cin, cout, lin, lout, res, part, acc,
    ag_send, ag_recv, y_send, x_send, x_recv, st_send, st_recv, p_send, p_recv, own_send, own_recv,
    pl_send, pl_recv, wp_send, wp_recv, nb_send, nb_recv,
    hid_send, hid_recv, c_send, c_recv, l_send, l_recv, res_send, res_recv,
):
    y = lax.axis_index("rows_0")
    x = lax.axis_index("rows_1")
    z = lax.axis_index("mp_0")
    c = lax.axis_index("mp_1")
    r = y * NP + x

    def dev(yy, xx, zz, cc):
        return (yy, xx, zz, cc)

    partner = dev(y, x, z, 1 - c)
    zup = dev(y, x, (z + 1) % NZ, c)
    zdn = dev(y, x, (z + NZ - 1) % NZ, c)
    zup2 = dev(y, x, (z + 2) % NZ, c)
    zdn2 = dev(y, x, (z + NZ - 2) % NZ, c)

    def remote(src, dst, ssem, rsem, to):
        return pltpu.make_async_remote_copy(
            src_ref=src, dst_ref=dst, send_sem=ssem, recv_sem=rsem,
            device_id=to, device_id_type=pl.DeviceIdType.MESH,
        )

    def signal_all(targets):
        bar = pltpu.get_barrier_semaphore()
        for t in targets:
            pl.semaphore_signal(bar, inc=1, device_id=t, device_id_type=pl.DeviceIdType.MESH)

    def wait_all(n):
        pl.semaphore_wait(pltpu.get_barrier_semaphore(), n)

    def peer(k, cc):
        return dev((y + k) % NP, x, z, cc)

    peers = [peer(k, cc) for k in (1, 2, 3) for cc in (0, 1)]

    @pl.when(c == 0)
    def _():
        signal_all([partner, dev(y, (x + 1) % NP, z, c), dev(y, (x + NP - 1) % NP, z, c)] + peers)

    @pl.when(c == 1)
    def _():
        signal_all([partner, zup, zdn, zup2, zdn2] + peers)


    def put_weight(src, dst):
        t = src[...].astype(F32).T.astype(BF16)
        dst[c, 2 * r] = t[0:HALF, :]
        dst[c, 2 * r + 1] = t[HALF:BLK, :]

    def spread_gain(t):
        row = gain_ref[pl.ds(12 * y + t, 1), :]
        gt[t] = jnp.broadcast_to(row, (128, 128)).T

    def bias_column():
        parts = [jnp.broadcast_to(bias_ref[k:k + 1, :], (128, 128)).T for k in range(3)]
        return jnp.concatenate(parts, axis=0)

    def get_stats(k):
        b = (y + k) % NP
        remote(st.at[b], st.at[b], st_send.at[0], st_recv.at[b], partner).wait_recv()

    def project(cc, ks):
        w = [w1[cc, pl.ds(2 * (NP * y + j), 2)].reshape(BLK, BLK) for j in range(NP)]
        for n, k in enumerate(ks):
            b = (y + k) % NP
            mean = st[b, 0, 0:1, :]
            inv = st[b, 1, 0:1, :]

            def norm(j, _):
                v = x4[b, pl.ds(2 * j, 2)].reshape(BLK, TOK).astype(F32)
                g = gt[pl.ds(3 * j, 3)].reshape(BLK, TOK)
                nx[j, :, TOK * n:TOK * n + TOK] = ((v - mean) * inv * g).astype(BF16)
                return 0

            lax.fori_loop(0, NP, norm, 0)
        total = jnp.dot(w[0], nx[0], preferred_element_type=F32)
        for j in range(1, NP):
            total = total + jnp.dot(w[j], nx[j], preferred_element_type=F32)
        return total

    def shares(cc):
        def give(k, v):
            b = (y + k) % NP
            pout[b] = v.astype(BF16)
            remote(pout.at[b], pin.at[y], p_send, p_recv.at[y], dev(b, x, z, cc)).start()

        v = project(cc, (2, 1))
        give(2, v[:, 0:TOK])
        give(1, v[:, TOK:])
        v = project(cc, (3, 0))
        give(3, v[:, 0:TOK])
        acc[...] = v[:, TOK:] + bias_column()

    def activate(cc):
        v = acc[...]
        for k in (1, 2, 3):
            b = (y + k) % NP
            remote(pout.at[b], pin.at[b], p_send, p_recv.at[b], partner).wait_recv()
            v = v + pin[b].astype(F32)
        hid[cc] = gelu(v).astype(BF16)

    @pl.when(c == 0)
    def _():
        weights = (w1, w2)

        def full(w, cc, b):
            return weights[w].at[cc, pl.ds(2 * b, 2)]

        def half(w, cc, b, h):
            return weights[w].at[cc, 2 * b + h]

        def axis(cc):
            if cc == 0:
                return x, y, (lambda p, q: q * NP + p), (lambda p, q: dev(q, p, z, c))
            return y, x, (lambda p, q: p * NP + q), (lambda p, q: dev(p, q, z, c))

        def send(w, cc, ref, idx, to):
            remote(ref, ref, pl_send.at[w, cc], pl_recv.at[w, cc, idx], to).start()

        def arrived(w, cc, ref, idx):
            remote(ref, ref, pl_send.at[w, cc], pl_recv.at[w, cc, idx], partner).wait_recv()

        def push(w, cc, b):
            ref = full(w, cc, b)
            remote(ref, ref, wp_send.at[w, cc], wp_recv.at[w, cc, b], partner).start()

        def mod(v):
            return (v + NP) % NP

        offs = (0, -1, 1, 2)

        def row_block(k):
            return NP * y + (x + k + NP) % NP

        def row_dev(k):
            return dev(y, (x + k + NP) % NP, z, c)

        def row_own():
            for cc in (0, 1):
                send(0, cc, full(0, cc, r), 0, row_dev(1))
                send(0, cc, full(0, cc, r), 1, row_dev(-1))

        def row_full():
            for cc in (0, 1):
                for d, k in ((0, -1), (1, 1)):
                    b = row_block(k)
                    arrived(0, cc, full(0, cc, b), d)
                    send(0, cc, half(0, cc, b, d), 2 + d, row_dev(-k))
                    if cc == 1:
                        push(0, cc, b)

        def row_half():
            for cc in (0, 1):
                b = row_block(2)
                arrived(0, cc, half(0, cc, b, 0), 2)
                arrived(0, cc, half(0, cc, b, 1), 3)
                if cc == 1:
                    push(0, cc, b)

        def own_sends():
            for cc in (1, 0):
                p, q, ident, at = axis(cc)
                send(1, cc, full(1, cc, r), 0, at(mod(p + 1), q))
                send(1, cc, full(1, cc, r), 1, at(mod(p - 1), q))
            for cc in (0, 1):
                q_sends(cc, 0, r)
            push(1, 0, r)

        def q_sends(cc, i, b):
            p, q, ident, at = axis(cc)
            send(1, cc, full(1, cc, b), 4 + 4 * i, at(p, mod(q + 1)))
            send(1, cc, full(1, cc, b), 5 + 4 * i, at(p, mod(q - 1)))

        def first_full(cc):
            for d, k in ((0, -1), (1, 1)):
                p, q, ident, at = axis(cc)
                b = ident(mod(p + k), q)
                arrived(1, cc, full(1, cc, b), d)
                send(1, cc, half(1, cc, b, d), 2 + d, at(mod(p - k), q))
                q_sends(cc, 1 + d, b)
                push(1, cc, b)

        def first_half(cc):
            p, q, ident, at = axis(cc)
            b = ident(mod(p + 2), q)
            arrived(1, cc, half(1, cc, b, 0), 2)
            arrived(1, cc, half(1, cc, b, 1), 3)
            q_sends(cc, 3, b)
            push(1, cc, b)

        def second_full(cc, i):
            for d, k in ((0, -1), (1, 1)):
                p, q, ident, at = axis(cc)
                b = ident(mod(p + offs[i]), mod(q + k))
                arrived(1, cc, full(1, cc, b), 4 + 4 * i + d)
                send(1, cc, half(1, cc, b, d), 6 + 4 * i + d, at(p, mod(q - k)))
                push(1, cc, b)

        def second_half(cc, i):
            p, q, ident, at = axis(cc)
            b = ident(mod(p + offs[i]), mod(q + 2))
            arrived(1, cc, half(1, cc, b, 0), 6 + 4 * i)
            arrived(1, cc, half(1, cc, b, 1), 7 + 4 * i)
            push(1, cc, b)

        wait_all(9)
        remote(tok_ref, xt.at[z, 0], own_send, own_recv, partner).start()
        put_weight(win_ref, w1)
        remote(full(0, 1, r), full(0, 1, r), nb_send.at[0], nb_recv.at[0], partner).wait_recv()
        row_own()
        put_weight(wout_ref, w2)
        remote(full(1, 1, r), full(1, 1, r), nb_send.at[1], nb_recv.at[1], partner).wait_recv()
        own_sends()
        lax.fori_loop(0, 12, lambda t, _: (spread_gain(t), 0)[1], 0)
        first_full(1)
        second_full(0, 0)
        row_full()
        first_half(1)
        first_full(0)
        second_full(1, 0)
        row_half()
        first_half(0)
        for i in (1, 2):
            second_full(0, i)
            second_full(1, i)
        second_half(0, 0)
        second_half(1, 0)
        second_full(0, 3)
        second_full(1, 3)

        def take(j, _):
            for b in range(NP):
                for h in (0, 1):
                    ref = x4.at[b, j, h]
                    remote(ref, ref, x_send, x_recv.at[b, j, h], partner).wait_recv()
            return 0

        lax.fori_loop(0, 8, take, 0)
        for k in range(NP):
            get_stats(k)
        shares(0)
        for i in (1, 2, 3):
            second_half(0, i)
            second_half(1, i)
        activate(0)
        remote(hid.at[0], hid.at[0], hid_send, hid_recv, partner).start()

        for cc in (0, 1):
            ref = w1.at[cc, pl.ds(0, 6)]
            remote(ref, ref, pl_send.at[0, cc], pl_recv.at[0, cc, 0], partner).wait_send()
            ref = w2.at[cc, pl.ds(0, 30)]
            remote(ref, ref, pl_send.at[1, cc], pl_recv.at[1, cc, 0], partner).wait_send()
            ref = w2.at[cc, pl.ds(0, 32 - 2 * cc)]
            remote(ref, ref, wp_send.at[1, cc], wp_recv.at[1, cc, 0], partner).wait_send()
        ref = w1.at[1, pl.ds(0, 6)]
        remote(ref, ref, wp_send.at[0, 1], wp_recv.at[0, 1, 0], partner).wait_send()
        remote(pout.at[pl.ds(0, 3)], pout.at[pl.ds(0, 3)], p_send, own_recv, partner).wait_send()
        remote(tok_ref, xt.at[z, 0], own_send, own_recv, partner).wait_send()
        remote(hid.at[0], hid.at[0], hid_send, hid_recv, partner).wait_send()
        remote(res.at[0], res.at[0], res_send, res_recv, partner).wait_recv()
        out_ref[...] = res[0]

    @pl.when(c == 1)
    def _():
        own1 = xt.at[z, 1]
        own0 = xt.at[z, 0]
        xt[z, 1] = tok_ref[...]
        sums[...] = jnp.zeros((2, 8, TOK), F32)
        wait_all(11)

        def pass_on(src, a, h, dr, s):
            ref = xt.at[a, h]
            remote(src, ref, ag_send, ag_recv.at[dr, s + 2, h], (zup2, zdn2)[dr]).start()
            remote(src, ref, ag_send, ag_recv.at[dr, s + 1, h], (zup, zdn)[dr]).start()

        pass_on(tok_ref, z, 1, 0, 0)
        pass_on(tok_ref, z, 1, 1, 0)

        def deliver(a, h):
            g = a // 8
            k = a % 8

            @pl.when(g != y)
            def _():
                remote(xt.at[a, h], x4.at[y, k, h], y_send, x_recv.at[y, k, h], dev(g, x, z, 1)).start()

            @pl.when(g == y)
            def _():
                remote(xt.at[a, h], x4.at[y, k, h], x_send, x_recv.at[y, k, h], partner).start()
                x4[y, k, h] = xt[a, h]

            v = xt[a, h].astype(F32).reshape(FEAT // 8, 8, TOK)
            sums[0] = sums[0] + jnp.sum(v, axis=0)
            sums[1] = sums[1] + jnp.sum(v * v, axis=0)

        def relay(a):
            @pl.when(a // 8 == y)
            def _():
                for k in (1, 2, 3):
                    b = (y + k) % NP
                    for h in (1, 0):
                        ref = x4.at[b, a % 8, h]
                        remote(ref, ref, x_send, x_recv.at[b, a % 8, h], partner).wait_recv()
                        remote(ref, ref, x_send, x_recv.at[b, a % 8, h], partner).start()

        put_weight(win_ref, w1)
        wb = w1.at[1, pl.ds(2 * r, 2)]
        remote(wb, wb, nb_send.at[0], nb_recv.at[0], partner).start()
        deliver(z, 1)
        remote(own0, own0, own_send, own_recv, partner).wait_recv()
        pass_on(own0, z, 0, 0, 0)
        pass_on(own0, z, 0, 1, 0)
        put_weight(wout_ref, w2)
        wo = w2.at[1, pl.ds(2 * r, 2)]
        remote(wo, wo, nb_send.at[1], nb_recv.at[1], partner).start()
        deliver(z, 0)

        def came(dr, a, s, h):
            ref = xt.at[a, h]
            remote(ref, ref, ag_send, ag_recv.at[dr, s, h], zup).wait_recv()

        def relays(i):
            relay((z + NZ - 2 * i) % NZ)
            relay((z + NZ - 2 * i + 1) % NZ)
            relay((z + 2 * i - 1) % NZ)

            @pl.when(i < PAIRS)
            def _():
                relay((z + 2 * i) % NZ)

        def ring(i, _):
            a = (z + NZ - 2 * i) % NZ
            b = (z + 2 * i) % NZ
            a1 = (z + NZ - 2 * i + 1) % NZ
            b1 = (z + 2 * i - 1) % NZ
            for h in (1, 0):
                came(0, a, 2 * i, h)

                @pl.when(i < PAIRS)
                def _():
                    pass_on(xt.at[a, h], a, h, 0, 2 * i)
                    came(1, b, 2 * i, h)

                    @pl.when(i < PAIRS - 1)
                    def _():
                        remote(xt.at[b, h], xt.at[b, h], ag_send, ag_recv.at[1, 2 * i + 2, h], zdn2).start()

                    remote(xt.at[b, h], xt.at[b, h], ag_send, ag_recv.at[1, 2 * i + 1, h], zdn).start()

            for h in (1, 0):
                came(0, a1, 2 * i - 1, h)
                deliver(a1, h)
                came(1, b1, 2 * i - 1, h)
                deliver(b1, h)
                deliver(a, h)

                @pl.when(i < PAIRS)
                def _():
                    deliver(b, h)

            @pl.when(i == 2)
            def _():
                relay(z)

            @pl.when(i > 2)
            def _():
                relays(i - 2)

            @pl.when(i <= 6)
            def _():
                spread_gain(2 * i - 2)
                spread_gain(2 * i - 1)

            return 0

        lax.fori_loop(1, PAIRS + 1, ring, 0)
        mean = jnp.sum(sums[0], axis=0, keepdims=True) / WIDTH
        var = jnp.maximum(jnp.sum(sums[1], axis=0, keepdims=True) / WIDTH - mean * mean, 0.0)
        st[y, 0] = jnp.broadcast_to(mean, (8, TOK))
        st[y, 1] = jnp.broadcast_to(lax.rsqrt(var + floor_value), (8, TOK))
        for n, to in enumerate(peers + [partner]):
            remote(st.at[y], st.at[y], st_send.at[n], st_recv.at[y], to).start()
        relays(PAIRS - 1)
        relays(PAIRS)

        def take_weight(k, _):
            b = NP * y + (x + k) % NP
            ref = w1.at[1, pl.ds(2 * b, 2)]
            remote(ref, ref, wp_send.at[0, 1], wp_recv.at[0, 1, b], partner).wait_recv()
            return 0

        lax.fori_loop(1, NP, take_weight, 0)
        for k in (1, 2, 3):
            get_stats(k)
        shares(1)
        activate(1)
        remote(hid.at[0], hid.at[0], hid_send, hid_recv, partner).wait_recv()

        def take_out(b):
            ra = w2.at[0, pl.ds(2 * b, 2)]
            remote(ra, ra, wp_send.at[1, 0], wp_recv.at[1, 0, b], partner).wait_recv()

            @pl.when(b != r)
            def _():
                rb = w2.at[1, pl.ds(2 * b, 2)]
                remote(rb, rb, wp_send.at[1, 1], wp_recv.at[1, 1, b], partner).wait_recv()

        def partial(d):
            return jnp.dot(w2[0, d], hid[0], preferred_element_type=F32) + jnp.dot(
                w2[1, d], hid[1], preferred_element_type=F32
            )

        def chain(dr, i, h):
            return remote(
                cout.at[dr, i, h], cin.at[dr, i, h], c_send.at[dr], c_recv.at[dr, i, h], (zup2, zdn2)[dr]
            )

        def link(dr, i):
            return remote(
                lout.at[dr, i], lin.at[dr, i], l_send.at[dr], l_recv.at[dr, i], (zup, zdn)[dr]
            )

        def lend(dr, i, d):
            v = partial(d).astype(BF16)
            lout[dr, i, 0] = v[0:FEAT]
            lout[dr, i, 1] = v[FEAT:HALF]
            link(dr, i).start()

        def carry(dr, i, h, terms):
            v = part[dr, FEAT * h:FEAT * h + FEAT]
            for t in terms:
                v = v + t.astype(F32)
            cout[dr, i, h] = v.astype(BF16)
            chain(dr, i, h).start()

        lax.fori_loop(0, NR, lambda b, _: (take_out(b), 0)[1], 0)
        part[0] = partial((z + STEPS) % NZ)
        carry(0, 0, 0, ())
        carry(0, 0, 1, ())
        lend(1, 0, (z + NZ - STEPS + 1) % NZ)
        lend(0, 0, (z + STEPS - 1) % NZ)
        part[1] = partial((z + NZ - STEPS + 2) % NZ)
        link(1, 0).wait_recv()
        carry(1, 0, 0, (lin[1, 0, 0],))
        carry(1, 0, 1, (lin[1, 0, 1],))

        def reduce(i, _):
            lend(1, i, (z + NZ - STEPS + 1 + 2 * i) % NZ)
            lend(0, i, (z + STEPS - 1 - 2 * i) % NZ)
            part[0] = partial((z + STEPS - 2 * i) % NZ)

            @pl.when(i < PAIRS - 1)
            def _():
                part[1] = partial((z + NZ - STEPS + 2 + 2 * i) % NZ)

            link(0, i - 1).wait_recv()
            link(1, i).wait_recv()
            for h in (0, 1):
                chain(0, i - 1, h).wait_recv()
                carry(0, i, h, (cin[0, i - 1, h], lin[0, i - 1, h]))

                @pl.when(i < PAIRS - 1)
                def _():
                    chain(1, i - 1, h).wait_recv()
                    carry(1, i, h, (cin[1, i - 1, h], lin[1, i, h]))

            return 0

        lax.fori_loop(1, PAIRS, reduce, 0)
        mine = partial(z)
        link(0, PAIRS - 1).wait_recv()
        for h in (0, 1):
            chain(0, PAIRS - 1, h).wait_recv()
            chain(1, PAIRS - 2, h).wait_recv()
            total = (
                xt[z, h].astype(F32)
                + mine[FEAT * h:FEAT * h + FEAT]
                + (cin[0, PAIRS - 1, h].astype(F32) + lin[0, PAIRS - 1, h].astype(F32))
                + (cin[1, PAIRS - 2, h].astype(F32) + lin[1, PAIRS - 1, h].astype(F32))
            )
            if h == 0:
                res[0] = total.astype(BF16)
                remote(res.at[0], res.at[0], res_send, res_recv, partner).start()
            else:
                out_ref[...] = total.astype(BF16)

        remote(xt.at[pl.ds(0, NZ - 1)], xt.at[pl.ds(0, NZ - 1)], ag_send, own_recv, partner).wait_send()
        remote(xt.at[pl.ds(0, 24)], xt.at[pl.ds(0, 24)], y_send, own_recv, partner).wait_send()
        remote(x4, x4, x_send, own_recv, partner).wait_send()
        for n in range(7):
            remote(st.at[y], st.at[y], st_send.at[n], own_recv, partner).wait_send()
        remote(pout.at[pl.ds(0, 3)], pout.at[pl.ds(0, 3)], p_send, own_recv, partner).wait_send()
        for w, ref in ((0, wb), (1, wo)):
            remote(ref, ref, nb_send.at[w], nb_recv.at[w], partner).wait_send()
        for dr, n in ((0, PAIRS), (1, PAIRS - 1)):
            ref = cout.at[dr, pl.ds(0, n)]
            remote(ref, ref, c_send.at[dr], own_recv, partner).wait_send()
            ref = lout.at[dr]
            remote(ref, ref, l_send.at[dr], own_recv, partner).wait_send()
        remote(res.at[0], res.at[0], res_send, res_recv, partner).wait_send()


def body(tokens, norm_gain, hidden_bias, weight_in, weight_out):
    dma = pltpu.SemaphoreType.DMA
    vmem = pl.BlockSpec(memory_space=pltpu.VMEM)
    return pl.pallas_call(
        kernel,
        out_shape=jax.ShapeDtypeStruct((FEAT, TOK), BF16),
        in_specs=[vmem] * 5,
        out_specs=vmem,
        scratch_shapes=[
            pltpu.VMEM((NZ, 2, FEAT, TOK), BF16),
            pltpu.VMEM((NP, 8, 2, FEAT, TOK), BF16),
            pltpu.VMEM((NP, BLK, 2 * TOK), BF16),
            pltpu.VMEM((2, NZ, HALF, BLK), BF16),
            pltpu.VMEM((2, NZ, HALF, BLK), BF16),
            pltpu.VMEM((12, 128, 128), F32),
            pltpu.VMEM((NP, 2, 8, TOK), F32),
            pltpu.VMEM((2, 8, TOK), F32),
            pltpu.VMEM((NP, BLK, TOK), BF16),
            pltpu.VMEM((NP, BLK, TOK), BF16),
            pltpu.VMEM((2, BLK, TOK), BF16),
            pltpu.VMEM((2, PAIRS, 2, FEAT, TOK), BF16),
            pltpu.VMEM((2, PAIRS, 2, FEAT, TOK), BF16),
            pltpu.VMEM((2, PAIRS, 2, FEAT, TOK), BF16),
            pltpu.VMEM((2, PAIRS, 2, FEAT, TOK), BF16),
            pltpu.VMEM((1, FEAT, TOK), BF16),
            pltpu.VMEM((2, HALF, TOK), F32),
            pltpu.VMEM((BLK, TOK), F32),
            dma, dma((2, STEPS + 1, 2)), dma, dma, dma((NP, 8, 2)), dma((7,)), dma((NP,)),
            dma, dma((NP,)), dma, dma,
            dma((2, 2)), dma((2, 2, 20)), dma((2, 2)), dma((2, 2, NR)), dma((2,)), dma((2,)),
            dma, dma, dma((2,)), dma((2, PAIRS, 2)), dma((2,)), dma((2, PAIRS)), dma, dma,
        ],
        compiler_params=pltpu.CompilerParams(
            collective_id=0, has_side_effects=True, vmem_limit_bytes=60 * 1024 * 1024
        ),
    )(
        tokens.T,
        norm_gain.reshape(48, 128),
        hidden_bias.reshape(3, 128),
        weight_in,
        weight_out,
    ).T


def solution(mesh):
    finer = Mesh(mesh.devices.reshape(4, 4, 32, 2), ("rows_0", "rows_1", "mp_0", "mp_1"))
    placed = (P(ROWS, MP), P(), P(MP), P(ROWS, MP), P(MP, ROWS))
    return jax.shard_map(body, mesh=finer, in_specs=placed, out_specs=P(ROWS, MP), check_vma=False)
```

time: 445 us -> 106 us (0.24)
  waiting for transfers between devices: 309 us -> 0 us
  Pallas kernels: 0 us -> 103 us
  blocking collectives: 100 us -> 0 us
  between operations: 14.6 us -> 0.01 us
  matrix products: 7.37 us -> 0 us
  local copies, waits for them, and re-layouts: 8.09 us -> 1.35 us
    reduce_scatter x4 -> x0, waiting for transfers between devices: 232 us -> none  [the longest x2 171 us: reduced_to_own(): parts = lax.psum_scatter(parts, axes[k], scatter_dimension=0, tiled=True)]
    pallas_call x0 -> x1, Pallas kernels: none -> 103 us  [body(): pl.pallas_call(kernel, out_shape=jax.ShapeDtypeStruct((FEAT, TOK), BF16),...]
    all_gather x2 -> x0, waiting for transfers between devices: 76.9 us -> none  [the longest x1 54.4 us: body(): lax.all_gather(weight_out, ROWS, axis=1, tiled=True)]
    all_gather x1 -> x0, blocking collectives: 72.8 us -> none  [all_blocks(): parts = lax.all_gather(parts, axes[k])]
    all_to_all x1 -> x0, blocking collectives: 27.7 us -> none  [body(): lax.all_to_all(normed, ROWS, split_axis=1, concat_axis=0, tiled=True)]
    dot_general x2 -> x0, matrix products: 7.37 us -> none  [the longest x1 4.62 us: body(): jnp.dot(hidden, lax.all_gather(weight_out, ROWS, axis=1, tiled=True), pre...]
  transfers between devices with their start and end apart: 6 -> 0, of which waited for: 6 -> 0; matrix products, arithmetic and copies ran while one was open for 0% -> 0% of each run, Pallas kernels for 0% -> 0%
where the time goes in v2:
time: 106 us; the launch traced here: 104 us
  Pallas kernels  103 us (97%)
  local copies, waits for them, and re-layouts  1.35 us (1%)
    pallas_call x1, Pallas kernels, body(): pl.pallas_call(kernel, out_shape=jax.ShapeDtypeStruct((FEAT, TOK), BF16),...  103 us

profile of v2, /device:TPU:6, one launch (start us, length us, event | category | flops | bytes accessed | tf_op | source)
XLA Modules:
  0.0 104.3 jit_solution(13161753756389008478)
XLA Ops:
  0.0 103.0 %shard_map.55 = bf16[96,128]{1,0:T(8,128)(2,1)} custom-call(bf16[96,128]{1,0:T(8,128)(2,1)} %bitcast.5, f32[48,128]{1,0:T(8,128)} %bitcast.6, f32[3,128]{1,0:T(4,128)} %bitcast.7, bf16[384,384]{1,0:T(8,128)(2,1)} %win_ref.1, bf16[384,384]{1,0:T(8,128)(2,1)} %wout_ref.1), custom_call_target="tpu_custom_call" | custom-call | tf_op jit(solution)/shard_map/pallas_call | solution.py:542
  103.0 1.3 %copy.7 = bf16[128,96]{0,1:T(8,128)(2,1)} copy(bf16[128,96]{0,1:T(8,128)(2,1)} %bitcast.4) | data formatting | bytes 49152

commit v3 on v2

--- a/solution.py
+++ b/solution.py
@@ -30,7 +30,7 @@
 
 def kernel(
     tok_ref, gain_ref, bias_ref, win_ref, wout_ref, out_ref,
-    xt, x4, nx, w1, w2, gt, st, sums, pout, pin, hid, cin, cout, lin, lout, res, part, acc,
+    xt, x4, nx, w1, w2, gt, st, sums, pout, pin, hid, cin, cout, lin, lout, res, part, acc, pout0, pin0,
     ag_send, ag_recv, y_send, x_send, x_recv, st_send, st_recv, p_send, p_recv, own_send, own_recv,
     pl_send, pl_recv, wp_send, wp_recv, nb_send, nb_recv,
     hid_send, hid_recv, c_send, c_recv, l_send, l_recv, res_send, res_recv,
@@ -114,18 +114,20 @@
             total = total + jnp.dot(w[j], nx[j], preferred_element_type=F32)
         return total
 
-    def shares(cc):
-        def give(k, v):
-            b = (y + k) % NP
-            pout[b] = v.astype(BF16)
-            remote(pout.at[b], pin.at[y], p_send, p_recv.at[y], dev(b, x, z, cc)).start()
-
+    def give(cc, k, v):
+        b = (y + k) % NP
+        pout[b] = v.astype(BF16)
+        remote(pout.at[b], pin.at[y], p_send, p_recv.at[y], dev(b, x, z, cc)).start()
+
+    def first_shares(cc):
         v = project(cc, (2, 1))
-        give(2, v[:, 0:TOK])
-        give(1, v[:, TOK:])
+        give(cc, 2, v[:, 0:TOK])
+        give(cc, 1, v[:, TOK:])
+
+    def last_shares(cc):
         v = project(cc, (3, 0))
-        give(3, v[:, 0:TOK])
-        acc[...] = v[:, TOK:] + bias_column()
+        give(cc, 3, v[:, 0:TOK])
+        acc[...] += v[:, TOK:]
 
     def activate(cc):
         v = acc[...]
@@ -157,6 +159,8 @@
             remote(ref, ref, pl_send.at[w, cc], pl_recv.at[w, cc, idx], partner).wait_recv()
 
         def push(w, cc, b):
+            if cc == 0:
+                return
             ref = full(w, cc, b)
             remote(ref, ref, wp_send.at[w, cc], wp_recv.at[w, cc, b], partner).start()
 
@@ -200,7 +204,6 @@
                 send(1, cc, full(1, cc, r), 1, at(mod(p - 1), q))
             for cc in (0, 1):
                 q_sends(cc, 0, r)
-            push(1, 0, r)
 
         def q_sends(cc, i, b):
             p, q, ident, at = axis(cc)
@@ -248,6 +251,7 @@
         remote(full(1, 1, r), full(1, 1, r), nb_send.at[1], nb_recv.at[1], partner).wait_recv()
         own_sends()
         lax.fori_loop(0, 12, lambda t, _: (spread_gain(t), 0)[1], 0)
+        acc[...] = bias_column()
         first_full(1)
         second_full(0, 0)
         row_full()
@@ -259,11 +263,6 @@
         for i in (1, 2):
             second_full(0, i)
             second_full(1, i)
-        second_half(0, 0)
-        second_half(1, 0)
-        second_full(0, 3)
-        second_full(1, 3)
-
         def take(j, _):
             for b in range(NP):
                 for h in (0, 1):
@@ -274,30 +273,55 @@
         lax.fori_loop(0, 8, take, 0)
         for k in range(NP):
             get_stats(k)
-        shares(0)
-        for i in (1, 2, 3):
+        first_shares(0)
+        last_shares(0)
+        second_full(0, 3)
+        second_full(1, 3)
+        activate(0)
+        for i in range(NP):
             second_half(0, i)
             second_half(1, i)
-        activate(0)
-        remote(hid.at[0], hid.at[0], hid_send, hid_recv, partner).start()
-
+
+        def hand(d):
+            d = (d + 2 * NZ) % NZ
+            pout0[d] = jnp.dot(w2[0, d], hid[0], preferred_element_type=F32)
+            remote(pout0.at[d], pin0.at[d], hid_send, hid_recv.at[d], partner).start()
+
+        def hand_step(i, _):
+            hand(z - STEPS + 1 + 2 * i)
+            hand(z + STEPS - 1 - 2 * i)
+            hand(z + STEPS - 2 * i)
+
+            @pl.when(i < PAIRS - 1)
+            def _():
+                hand(z - STEPS + 2 + 2 * i)
+
+            return 0
+
+        hand(z + STEPS)
+        hand(z - STEPS + 1)
+        hand(z + STEPS - 1)
+        hand(z - STEPS + 2)
+        lax.fori_loop(1, PAIRS, hand_step, 0)
+        hand(z)
         for cc in (0, 1):
             ref = w1.at[cc, pl.ds(0, 6)]
             remote(ref, ref, pl_send.at[0, cc], pl_recv.at[0, cc, 0], partner).wait_send()
             ref = w2.at[cc, pl.ds(0, 30)]
             remote(ref, ref, pl_send.at[1, cc], pl_recv.at[1, cc, 0], partner).wait_send()
-            ref = w2.at[cc, pl.ds(0, 32 - 2 * cc)]
-            remote(ref, ref, wp_send.at[1, cc], wp_recv.at[1, cc, 0], partner).wait_send()
+        ref = w2.at[1, pl.ds(0, 30)]
+        remote(ref, ref, wp_send.at[1, 1], wp_recv.at[1, 1, 0], partner).wait_send()
         ref = w1.at[1, pl.ds(0, 6)]
         remote(ref, ref, wp_send.at[0, 1], wp_recv.at[0, 1, 0], partner).wait_send()
         remote(pout.at[pl.ds(0, 3)], pout.at[pl.ds(0, 3)], p_send, own_recv, partner).wait_send()
         remote(tok_ref, xt.at[z, 0], own_send, own_recv, partner).wait_send()
-        remote(hid.at[0], hid.at[0], hid_send, hid_recv, partner).wait_send()
+        remote(pout0, pin0, hid_send, hid_recv.at[0], partner).wait_send()
         remote(res.at[0], res.at[0], res_send, res_recv, partner).wait_recv()
         out_ref[...] = res[0]
 
     @pl.when(c == 1)
     def _():
+        acc[...] = bias_column()
         own1 = xt.at[z, 1]
         own0 = xt.at[z, 0]
         xt[z, 1] = tok_ref[...]
@@ -394,13 +418,13 @@
                 def _():
                     deliver(b, h)
 
-            @pl.when(i == 2)
+            @pl.when(i == 4)
             def _():
                 relay(z)
 
-            @pl.when(i > 2)
-            def _():
-                relays(i - 2)
+            @pl.when(i > 4)
+            def _():
+                relays(i - 4)
 
             @pl.when(i <= 6)
             def _():
@@ -416,8 +440,8 @@
         st[y, 1] = jnp.broadcast_to(lax.rsqrt(var + floor_value), (8, TOK))
         for n, to in enumerate(peers + [partner]):
             remote(st.at[y], st.at[y], st_send.at[n], st_recv.at[y], to).start()
-        relays(PAIRS - 1)
-        relays(PAIRS)
+        for i in range(PAIRS - 3, PAIRS + 1):
+            relays(i)
 
         def take_weight(k, _):
             b = NP * y + (x + k) % NP
@@ -428,23 +452,20 @@
         lax.fori_loop(1, NP, take_weight, 0)
         for k in (1, 2, 3):
             get_stats(k)
-        shares(1)
+        first_shares(1)
+        last_shares(1)
         activate(1)
-        remote(hid.at[0], hid.at[0], hid_send, hid_recv, partner).wait_recv()
 
         def take_out(b):
-            ra = w2.at[0, pl.ds(2 * b, 2)]
-            remote(ra, ra, wp_send.at[1, 0], wp_recv.at[1, 0, b], partner).wait_recv()
-
             @pl.when(b != r)
             def _():
                 rb = w2.at[1, pl.ds(2 * b, 2)]
                 remote(rb, rb, wp_send.at[1, 1], wp_recv.at[1, 1, b], partner).wait_recv()
 
         def partial(d):
-            return jnp.dot(w2[0, d], hid[0], preferred_element_type=F32) + jnp.dot(
-                w2[1, d], hid[1], preferred_element_type=F32
-            )
+            v = jnp.dot(w2[1, d], hid[1], preferred_element_type=F32)
+            remote(pout0.at[d], pin0.at[d], hid_send, hid_recv.at[d], partner).wait_recv()
+            return v + pin0[d]
 
         def chain(dr, i, h):
             return remote(
@@ -469,7 +490,20 @@
             cout[dr, i, h] = v.astype(BF16)
             chain(dr, i, h).start()
 
-        lax.fori_loop(0, NR, lambda b, _: (take_out(b), 0)[1], 0)
+        def need(i):
+            odd = z % 2
+
+            @pl.when((i == 0) & (odd == 0))
+            def _():
+                take_out(((z + STEPS) % NZ) // 2)
+
+            take_out(((z + STEPS - 1 + odd - 2 * i) % NZ) // 2)
+
+            @pl.when((odd == 1) | (i < PAIRS - 1))
+            def _():
+                take_out(((z + NZ - STEPS + 2 - odd + 2 * i) % NZ) // 2)
+
+        need(0)
         part[0] = partial((z + STEPS) % NZ)
         carry(0, 0, 0, ())
         carry(0, 0, 1, ())
@@ -481,6 +515,7 @@
         carry(1, 0, 1, (lin[1, 0, 1],))
 
         def reduce(i, _):
+            need(i)
             lend(1, i, (z + NZ - STEPS + 1 + 2 * i) % NZ)
             lend(0, i, (z + STEPS - 1 - 2 * i) % NZ)
             part[0] = partial((z + STEPS - 2 * i) % NZ)
@@ -563,10 +598,12 @@
             pltpu.VMEM((1, FEAT, TOK), BF16),
             pltpu.VMEM((2, HALF, TOK), F32),
             pltpu.VMEM((BLK, TOK), F32),
+            pltpu.VMEM((NZ, HALF, TOK), F32),
+            pltpu.VMEM((NZ, HALF, TOK), F32),
             dma, dma((2, STEPS + 1, 2)), dma, dma, dma((NP, 8, 2)), dma((7,)), dma((NP,)),
             dma, dma((NP,)), dma, dma,
             dma((2, 2)), dma((2, 2, 20)), dma((2, 2)), dma((2, 2, NR)), dma((2,)), dma((2,)),
-            dma, dma, dma((2,)), dma((2, PAIRS, 2)), dma((2,)), dma((2, PAIRS)), dma, dma,
+            dma, dma((NZ,)), dma((2,)), dma((2, PAIRS, 2)), dma((2,)), dma((2, PAIRS)), dma, dma,
         ],
         compiler_params=pltpu.CompilerParams(
             collective_id=0, has_side_effects=True, vmem_limit_bytes=60 * 1024 * 1024

time: 106 us -> 106 us (level)
  no operation moved by 1% of the time
where the time goes in v3:
time: 106 us; the launch traced here: 104 us
  Pallas kernels  102 us (96%)
  local copies, waits for them, and re-layouts  1.35 us (1%)
    pallas_call x1, Pallas kernels, body(): pl.pallas_call(kernel, out_shape=jax.ShapeDtypeStruct((FEAT, TOK), BF16),...  102 us

profile of v3, /device:TPU:6, one launch (start us, length us, event | category | flops | bytes accessed | tf_op | source)
XLA Modules:
  0.0 103.8 jit_solution(4806496185751389517)
XLA Ops:
  0.0 102.4 %shard_map.55 = bf16[96,128]{1,0:T(8,128)(2,1)} custom-call(bf16[96,128]{1,0:T(8,128)(2,1)} %bitcast.5, f32[48,128]{1,0:T(8,128)} %bitcast.6, f32[3,128]{1,0:T(4,128)} %bitcast.7, bf16[384,384]{1,0:T(8,128)(2,1)} %win_ref.1, bf16[384,384]{1,0:T(8,128)(2,1)} %wout_ref.1), custom_call_target="tpu_custom_call" | custom-call | tf_op jit(solution)/shard_map/pallas_call | solution.py:577
  102.4 1.3 %copy.7 = bf16[128,96]{0,1:T(8,128)(2,1)} copy(bf16[128,96]{0,1:T(8,128)(2,1)} %bitcast.4) | data formatting | bytes 49152
